TPU v7x, 32 devices: a whole 2x2x4 slice. The times are simulated.
32 devices in a mesh: dp: 4 (over y, x), fsdp: 8 (over z, core).
Axes of the slice: x: 2, y: 2, z: 4, core: 2. Of those that a mesh axis runs over, the one named last changes fastest.
Arguments:
- input_tokens: int32 [2, 32768], P(None, ('dp', 'fsdp')), may hold values from 0 to 29
- item_numbers: int32 [2, 32768], P(None, ('dp', 'fsdp')), may hold values from -1 to 3, as said below
- loss_positions: int32 [2, 4096], P(None, ('dp', 'fsdp')), may hold values from -1 to 1023, as said below
- target_tokens: int32 [2, 4096], P(None, ('dp', 'fsdp')), may hold values from 0 to 29
- input_projection: float32 [1280, 640], P('fsdp', 'dp'), may hold values from -0.15625 to 0.15625
- dilated_conv: float32 [3200, 640], P('fsdp', 'dp'), may hold values from -0.109375 to 0.109375
- output_projection: float32 [1280, 640], P('fsdp', 'dp'), may hold values from -0.25 to 0.25
- vectors: float32 [68, 1280], P(None, ('dp', 'fsdp'))
- input_first_moment: float32 [1280, 640], P('fsdp'), may hold values from -6.67572e-06 to 6.67572e-06
- input_second_moment: float32 [1280, 640], P('fsdp'), may hold values from 5.3002034e-12 to 2.1200814e-11
- conv_first_moment: float32 [3200, 640], P('fsdp'), may hold values from -6.67572e-06 to 6.67572e-06
- conv_second_moment: float32 [3200, 640], P('fsdp'), may hold values from 5.3002034e-12 to 2.1200814e-11
- output_first_moment: float32 [1280, 640], P('fsdp'), may hold values from -6.67572e-06 to 6.67572e-06
- output_second_moment: float32 [1280, 640], P('fsdp'), may hold values from 5.3002034e-12 to 2.1200814e-11
- vector_first_moment: float32 [68, 1280], P(None, ('dp', 'fsdp')), may hold values from -1.9073486e-05 to 1.9073486e-05
- vector_second_moment: float32 [68, 1280], P(None, ('dp', 'fsdp')), may hold values from 4.7701832e-11 to 1.9080733e-10
- bases: float32 [3, 640, 640], replicated, as said below
- eigenbasis_flags: int32 [3], replicated, may hold values from 0 to 1, as said below
- optimizer_step: int32 [1], replicated, may hold values from 2 to 20
Outputs:
- mean_loss: float32 [], replicated
- grad_norm: float32 [], replicated
- master_in: float32 [1280, 640], P('fsdp', 'dp')
- copy_in: bfloat16 [1280, 640], P('fsdp', 'dp')
- moment_in: float32 [1280, 640], P('fsdp')
- square_in: float32 [1280, 640], P('fsdp')
- updated_conv: float32 [3200, 640], P('fsdp', 'dp')
- conv_bfloat_copy: bfloat16 [3200, 640], P('fsdp', 'dp')
- updated_conv_moment: float32 [3200, 640], P('fsdp')
- updated_conv_square: float32 [3200, 640], P('fsdp')
- master_out: float32 [1280, 640], P('fsdp', 'dp')
- copy_out: bfloat16 [1280, 640], P('fsdp', 'dp')
- moment_out: float32 [1280, 640], P('fsdp')
- square_out: float32 [1280, 640], P('fsdp')
- master_vec: float32 [68, 1280], P(None, ('dp', 'fsdp'))
- copy_vec: bfloat16 [68, 1280], P(None, ('dp', 'fsdp'))
- moment_vec: float32 [68, 1280], P(None, ('dp', 'fsdp'))
- square_vec: float32 [68, 1280], P(None, ('dp', 'fsdp'))
Inputs may be any that keep to these rules, and one draw needn't show every extreme that they name: `item_numbers`: each device's 1024 slots of a micro-batch hold whole items of 256, 512 or 1024 tokens, numbered from 0 in order and starting at slot 0, followed by padding marked -1; items fill at least half of the slots; some device holds one item of 1024 tokens. `loss_positions`: slot i of a device's 128 slots in a micro-batch holds -1 or a position from 8 i to 8 i + 7 of that device's slots; it holds a position exactly when that position belongs to an item. `eigenbasis_flags`: two of the three entries are 1. `bases`: each matrix is orthogonal.
All inputs are finite; a program needn't handle non-finite values.
Results may differ from a plain program's by a relative error of at most 0.0091.
Values may be sent and summed in bfloat16 or wider, within the bound.
A program may use at most 256 MiB of HBM per device.

v0:
```python
from functools import partial
import jax
import jax.numpy as jnp
from jax import lax
from jax.sharding import PartitionSpec as P

VOCAB = 30
CONV_TAPS = 5
DILATION = 8
TABLE = 32
beta_one = 0.9
beta_two = 0.95
epsilon = 1e-08
rate_matrix = 0.02
rate_vector = 0.5
decay_weight = 0.01
clip_limit = 0.02
norm_eps = 1e-05
highest_precision = lax.Precision.HIGHEST


def layer_norm(values, norm_gain, norm_bias):
    centre = values - jnp.mean(values, axis=-1, keepdims=True)
    spread = jnp.mean(centre * centre, axis=-1, keepdims=True)
    return centre * lax.rsqrt(spread + norm_eps) * norm_gain + norm_bias


def norm_gelu(values, norm_gain, norm_bias):
    return jax.nn.gelu(layer_norm(values, norm_gain, norm_bias), approximate=True)


def slot_loss(logits, labels, valid_slot):
    log_total = jax.nn.logsumexp(logits, axis=-1)
    hits = labels[:, None] == jnp.arange(logits.shape[1], dtype=jnp.int32)[None, :]
    chosen = jnp.sum(jnp.where(hits, logits, 0.0), axis=-1)
    return jnp.sum(jnp.where(valid_slot, log_total - chosen, 0.0))


def moved_groups(values, step):
    if step > 0:
        return jnp.concatenate([values[:, step:], jnp.full_like(values[:, :step], -1)], axis=1)
    if step < 0:
        return jnp.concatenate([jnp.full_like(values[:, :-step], -1), values[:, :step]], axis=1)
    return values


def tap_onehots(tokens, items, positions):
    batches, slots = positions.shape
    stride = tokens.shape[1] // slots
    token_groups = tokens.reshape(batches, slots, stride)
    item_groups = items.reshape(batches, slots, stride)
    valid = positions >= 0
    residue = jnp.where(valid, positions - stride * jnp.arange(slots, dtype=jnp.int32)[None], -1)
    chosen = residue[:, :, None] == jnp.arange(stride, dtype=jnp.int32)[None, None]
    own_item = jnp.sum(jnp.where(chosen, item_groups, 0), axis=2)
    identities = jnp.arange(TABLE, dtype=jnp.int32)
    result = []
    for tap in range(CONV_TAPS):
        step = (tap - CONV_TAPS // 2) * DILATION // stride
        item = jnp.sum(jnp.where(chosen, moved_groups(item_groups, step), 0), axis=2)
        token = jnp.sum(jnp.where(chosen, moved_groups(token_groups, step), 0), axis=2)
        keep = valid & (item == own_item) & (own_item >= 0)
        result.append(jnp.where(keep, token, -1)[:, :, None] == identities)
    return jnp.concatenate(result, axis=2).reshape(batches * slots, CONV_TAPS * TABLE)


def exact_dot(left, right, contract):
    high = left.astype(jnp.bfloat16)
    low = (left - high.astype(jnp.float32)).astype(jnp.bfloat16)
    return lax.dot_general(
        high, right, contract, preferred_element_type=jnp.float32
    ) + lax.dot_general(low, right, contract, preferred_element_type=jnp.float32)


def column_sum(values):
    return jnp.sum(values, axis=0, dtype=jnp.float32)


def gathered_weights(shards):
    parted = (
        lax.all_gather(shards[0], "fsdp", axis=0, tiled=True),
        lax.all_gather(shards[1], "fsdp", axis=0, tiled=True),
        lax.all_gather(shards[2], "fsdp", axis=0, tiled=True),
        lax.all_gather(shards[3], "fsdp", axis=1, tiled=True),
    )
    return (
        lax.all_gather(parted[0], "dp", axis=1, tiled=True),
        lax.all_gather(parted[1], "dp", axis=1, tiled=True),
        lax.all_gather(parted[2], "dp", axis=1, tiled=True),
        lax.all_gather(parted[3], "dp", axis=1, tiled=True),
    )


def eigenbasis_update(
    gradient, master, moment, square, rotated_grads, col_start, first_correction, second_correction
):
    rotated = jnp.dot(gradient, rotated_grads, precision=highest_precision)
    moment_new = beta_one * moment + (1.0 - beta_one) * rotated
    square_new = beta_two * square + (1.0 - beta_two) * rotated * rotated
    step_ratio = (
        moment_new / first_correction / (jnp.sqrt(square_new / second_correction) + epsilon)
    )
    own_basis = lax.dynamic_slice_in_dim(rotated_grads, col_start, master.shape[1], 0)
    update = jnp.einsum("ri,ci->rc", step_ratio, own_basis, precision=highest_precision)
    master_new = master - rate_matrix * (update + decay_weight * master)
    return (master_new, master_new.astype(jnp.bfloat16), moment_new, square_new)


def adam_vectors(gradient, master, moment, square, first_correction, second_correction):
    decay_rows = jnp.where(
        jnp.arange(master.shape[0], dtype=jnp.int32)[:, None] < 2 * VOCAB, decay_weight, 0.0
    )
    moment_new = beta_one * moment + (1.0 - beta_one) * gradient
    square_new = beta_two * square + (1.0 - beta_two) * gradient * gradient
    step_ratio = (
        moment_new / first_correction / (jnp.sqrt(square_new / second_correction) + epsilon)
    )
    master_new = master - rate_vector * (step_ratio + decay_rows * master)
    return (master_new, master_new.astype(jnp.bfloat16), moment_new, square_new)


def local(
    input_tokens,
    item_numbers,
    loss_positions,
    target_tokens,
    input_projection,
    dilated_conv,
    output_projection,
    vectors,
    input_first_moment,
    input_second_moment,
    conv_first_moment,
    conv_second_moment,
    output_first_moment,
    output_second_moment,
    vector_first_moment,
    vector_second_moment,
    bases,
    eigenbasis_flags,
    optimizer_step,
):
    shards_low = (
        input_projection.astype(jnp.bfloat16),
        dilated_conv.astype(jnp.bfloat16),
        output_projection.astype(jnp.bfloat16),
        vectors.astype(jnp.bfloat16),
    )
    weight_in, weight_conv, weight_out, table_low = gathered_weights(shards_low)
    groups, col_index = (lax.axis_size("dp"), lax.axis_index("dp"))
    rows, row_index = (lax.axis_size("fsdp"), lax.axis_index("fsdp"))
    inner = weight_in.shape[1]
    width = weight_in.shape[0]
    start = 2 * VOCAB
    table = table_low.astype(jnp.float32)
    head = table_low[VOCAB:start]
    onehots = tap_onehots(input_tokens, item_numbers, loss_positions)
    onehots_low = onehots.astype(jnp.bfloat16)
    centre = CONV_TAPS // 2 * TABLE
    centre_low = onehots_low[:, centre : centre + TABLE]
    embedded = jnp.concatenate(
        [table_low[:VOCAB], jnp.zeros((TABLE - VOCAB, width), jnp.bfloat16)], axis=0
    )
    first_act, first_back = jax.vjp(
        norm_gelu, embedded.astype(jnp.float32), table[start], table[start + 1]
    )
    first_low = first_act.astype(jnp.bfloat16)
    pre_inner = (
        jnp.dot(first_low, weight_in, preferred_element_type=jnp.float32) + table[start + 6, :inner]
    )
    second_act, second_back = jax.vjp(
        norm_gelu, pre_inner, table[start + 5, :inner], table[start + 5, inner:]
    )
    second_low = second_act.astype(jnp.bfloat16)
    picked_act = [
        jnp.dot(
            onehots_low[:, tap * TABLE : (tap + 1) * TABLE],
            second_low,
            preferred_element_type=jnp.float32,
        ).astype(jnp.bfloat16)
        for tap in range(CONV_TAPS)
    ]
    conv_input = (
        jnp.dot(
            jnp.concatenate(picked_act, axis=1), weight_conv, preferred_element_type=jnp.float32
        )
        + table[start + 6, inner:]
    )
    third_act, third_back = jax.vjp(
        norm_gelu, conv_input, table[start + 7, :inner], table[start + 7, inner:]
    )
    third_low = third_act.astype(jnp.bfloat16)
    branch = (
        jnp.einsum("ti,di->td", third_low, weight_out, preferred_element_type=jnp.float32)
        + table[start + 2]
    )
    picked_embedded = jnp.dot(centre_low, embedded, preferred_element_type=jnp.float32)
    final_out, final_back = jax.vjp(
        layer_norm, picked_embedded + branch, table[start + 3], table[start + 4]
    )
    picked = final_out.astype(jnp.bfloat16)
    logits = jnp.einsum("pd,vd->pv", picked, head, preferred_element_type=jnp.float32)
    valid = loss_positions.reshape(-1) >= 0
    summed_loss, loss_back = jax.vjp(
        partial(slot_loss, labels=target_tokens.reshape(-1), valid_slot=valid), logits
    )
    logit_grad = loss_back(jnp.ones((), jnp.float32))[0].astype(jnp.bfloat16)
    head_grad = jnp.einsum("pv,pd->vd", logit_grad, picked, preferred_element_type=jnp.float32)
    picked_grad = jnp.dot(logit_grad, head, preferred_element_type=jnp.float32)
    sum_grad, gain_four, bias_four = final_back(picked_grad)
    branch_low = sum_grad.astype(jnp.bfloat16)
    out_grad = jnp.einsum("td,ti->di", branch_low, third_low, preferred_element_type=jnp.float32)
    third_grad = jnp.dot(branch_low, weight_out, preferred_element_type=jnp.float32)
    conv_pre, gain_three, bias_three = third_back(third_grad)
    conv_low = conv_pre.astype(jnp.bfloat16)
    tap_grads = lax.dot_general(
        onehots_low, conv_low, (((0,), (0,)), ((), ())), preferred_element_type=jnp.float32
    )
    start_grads = jnp.einsum(
        "tv,td->vd", centre_low.astype(jnp.float32), sum_grad, precision=highest_precision
    )
    slot_count = jnp.sum(valid.astype(jnp.float32))
    wide_rows = jnp.concatenate(
        [
            start_grads[:VOCAB],
            head_grad,
            jnp.stack(
                [
                    column_sum(branch_low),
                    gain_four,
                    bias_four,
                    jnp.concatenate([gain_three, bias_three]),
                ]
            ),
        ],
        axis=0,
    )
    out_rows = lax.psum(
        lax.psum_scatter(out_grad.astype(jnp.bfloat16), "fsdp", scatter_dimension=0, tiled=True),
        "dp",
    ).astype(jnp.float32)
    tap_grads, wide_rows, summed_loss, slot_count = lax.psum(
        (tap_grads, wide_rows, summed_loss, slot_count), ("dp", "fsdp")
    )
    tap_view = tap_grads.reshape(CONV_TAPS, TABLE, inner)
    second_grad = sum(
        (
            exact_dot(
                tap_view[tap],
                weight_conv[tap * inner : (tap + 1) * inner],
                (((1,), (1,)), ((), ())),
            )
            for tap in range(CONV_TAPS)
        )
    )
    inner_pre, gain_two, bias_two = second_back(second_grad)
    first_grad = exact_dot(inner_pre, weight_in, (((1,), (1,)), ((), ())))
    table_grad, gain_one, bias_one = first_back(first_grad)
    vec_sum = jnp.concatenate(
        [
            table_grad[:VOCAB] + wide_rows[:VOCAB],
            wide_rows[VOCAB:start],
            jnp.stack(
                [
                    gain_one,
                    bias_one,
                    wide_rows[start],
                    wide_rows[start + 1],
                    wide_rows[start + 2],
                    jnp.concatenate([gain_two, bias_two]),
                    jnp.concatenate(
                        [jnp.sum(inner_pre, axis=0), jnp.sum(tap_view[CONV_TAPS // 2], axis=0)]
                    ),
                    wide_rows[start + 3],
                ]
            ),
        ],
        axis=0,
    )
    own = width // (groups * rows)
    vec_own = lax.dynamic_slice_in_dim(vec_sum, (col_index * rows + row_index) * own, own, 1)
    row_low = lax.dynamic_slice_in_dim(first_low, row_index * (width // rows), width // rows, 1)
    in_rows = jnp.einsum(
        "vr,vi->ri", row_low.astype(jnp.float32), inner_pre, precision=highest_precision
    )
    placed = (
        jnp.eye(CONV_TAPS, dtype=jnp.bfloat16)[:, None, :, None] * second_low[None, :, None, :]
    ).reshape(CONV_TAPS * TABLE, CONV_TAPS * inner)
    conv_count = CONV_TAPS * inner // rows
    conv_low_rows = lax.dynamic_slice_in_dim(placed, row_index * conv_count, conv_count, 1)
    conv_rows = jnp.einsum(
        "vr,vi->ri", conv_low_rows.astype(jnp.float32), tap_grads, precision=highest_precision
    )
    col_width = input_projection.shape[1]
    col_start = col_index * col_width
    owned = [
        lax.dynamic_slice_in_dim(full_rows, col_start, col_width, 1)
        for full_rows in (in_rows, conv_rows, out_rows)
    ]
    square_local = sum((jnp.sum(piece * piece) for piece in owned)) + jnp.sum(vec_own * vec_own)
    square_total = lax.psum(square_local, ("dp", "fsdp"))
    grad_norm = jnp.sqrt(square_total) / slot_count
    factor = jnp.minimum(1.0, clip_limit / grad_norm) / slot_count
    step_value = optimizer_step[0].astype(jnp.float32)
    first_correction = 1.0 - beta_one**step_value
    second_correction = 1.0 - beta_two**step_value
    identity = jnp.eye(bases.shape[1], dtype=jnp.float32)
    rotated_grads = [
        jnp.where(eigenbasis_flags[mat_index] == 1, bases[mat_index], identity)
        for mat_index in range(3)
    ]
    master_in, copy_in, moment_in, square_in = eigenbasis_update(
        in_rows * factor,
        input_projection,
        input_first_moment,
        input_second_moment,
        rotated_grads[0],
        col_start,
        first_correction,
        second_correction,
    )
    updated_conv, conv_bfloat_copy, updated_conv_moment, updated_conv_square = eigenbasis_update(
        conv_rows * factor,
        dilated_conv,
        conv_first_moment,
        conv_second_moment,
        rotated_grads[1],
        col_start,
        first_correction,
        second_correction,
    )
    master_out, copy_out, moment_out, square_out = eigenbasis_update(
        out_rows * factor,
        output_projection,
        output_first_moment,
        output_second_moment,
        rotated_grads[2],
        col_start,
        first_correction,
        second_correction,
    )
    master_vec, copy_vec, moment_vec, square_vec = adam_vectors(
        vec_own * factor,
        vectors,
        vector_first_moment,
        vector_second_moment,
        first_correction,
        second_correction,
    )
    return (
        summed_loss / slot_count,
        grad_norm,
        master_in,
        copy_in,
        moment_in,
        square_in,
        updated_conv,
        conv_bfloat_copy,
        updated_conv_moment,
        updated_conv_square,
        master_out,
        copy_out,
        moment_out,
        square_out,
        master_vec,
        copy_vec,
        moment_vec,
        square_vec,
    )


def solution(mesh):
    placed = (
        P(None, ("dp", "fsdp")),
        P(None, ("dp", "fsdp")),
        P(None, ("dp", "fsdp")),
        P(None, ("dp", "fsdp")),
        P("fsdp", "dp"),
        P("fsdp", "dp"),
        P("fsdp", "dp"),
        P(None, ("dp", "fsdp")),
        P("fsdp", None),
        P("fsdp", None),
        P("fsdp", None),
        P("fsdp", None),
        P("fsdp", None),
        P("fsdp", None),
        P(None, ("dp", "fsdp")),
        P(None, ("dp", "fsdp")),
        P(),
        P(),
        P(),
    )
    return jax.shard_map(
        local,
        mesh=mesh,
        in_specs=placed,
        out_specs=(
            P(),
            P(),
            P("fsdp", "dp"),
            P("fsdp", "dp"),
            P("fsdp", None),
            P("fsdp", None),
            P("fsdp", "dp"),
            P("fsdp", "dp"),
            P("fsdp", None),
            P("fsdp", None),
            P("fsdp", "dp"),
            P("fsdp", "dp"),
            P("fsdp", None),
            P("fsdp", None),
            P(None, ("dp", "fsdp")),
            P(None, ("dp", "fsdp")),
            P(None, ("dp", "fsdp")),
            P(None, ("dp", "fsdp")),
        ),
        check_vma=False,
    )
```

profile of v0, /device:TPU:0, one launch (start us, length us, event | category | flops | bytes accessed | tf_op | source)
XLA Modules:
  0.0 448.6 jit_solution(13318790857752670244)
XLA Ops:
  8.2 17.0 %all_gather.26 = bf16[1280,160]{1,0:T(8,128)(2,1)S(1)} all-gather(bf16[160,160]{1,0:T(8,128)(2,1)S(1)} %convert_element_type.159), channel_id=1, replica_groups=mesh['dp'=4,'fsdp'=8] {'fsdp'}, dimensions={0}, use_global_device_ids=true | all-gather | bytes 460800 | tf_op jit(solution)/shard_map/all_gather | solution.py:81
  26.2 19.0 %all-gather.1 = bf16[8,400,160]{1,2,0:T(8,128)(2,1)S(1)} all-gather(bf16[1,400,160]{1,2,0:T(8,128)(2,1)S(1)} %convert_bitcast_fusion), channel_id=1, replica_groups=mesh['dp'=4,'fsdp'=8] {'fsdp'}, dimensions={0}, use_global_device_ids=true | all-gather | bytes 1152000 | tf_op jit(solution)/shard_map/all_gather | solution.py:82
  46.0 2.4 reshape.268
  48.5 15.1 %all_gather.30 = bf16[1280,160]{1,0:T(8,128)(2,1)S(1)} all-gather(bf16[160,160]{1,0:T(8,128)(2,1)S(1)} %convert_element_type.168), channel_id=1, replica_groups=mesh['dp'=4,'fsdp'=8] {'fsdp'}, dimensions={0}, use_global_device_ids=true | all-gather | bytes 460800 | tf_op jit(solution)/shard_map/all_gather | solution.py:83
  65.4 13.9 %all_gather.24 = bf16[68,320]{0,1:T(8,128)(2,1)S(1)} all-gather(bf16[68,40]{0,1:T(8,128)(2,1)S(1)} %convert_element_type.155), channel_id=1, replica_groups=mesh['dp'=4,'fsdp'=8] {'fsdp'}, dimensions={1}, use_global_device_ids=true | all-gather | bytes 48960 | tf_op jit(solution)/shard_map/all_gather | solution.py:84
  79.4 9.3 %all-gather = bf16[4,320,68]{1,2,0:T(8,128)(2,1)S(1)} all-gather(bf16[1,320,68]{1,2,0:T(8,128)(2,1)S(1)} %copy.91), channel_id=1, replica_groups=mesh['dp'=4,'fsdp'=8] {'dp'}, dimensions={0}, use_global_device_ids=true | all-gather | bytes 217600 | tf_op jit(solution)/shard_map/all_gather | solution.py:90
  89.0 1.8 slice_reduce_fusion.1
  90.9 1.1 slice_reduce_fusion.6
  98.2 4.6 %convert_select_fusion = (f32[640,640]{1,0:T(8,128)}, f32[640,640]{1,0:T(8,128)}, f32[640,640]{1,0:T(8,128)S(1)}) fusion(f32[3,640,640]{2,1,0:T(8,128)} %param.35, pred[]{:T(512)} %bitcast.22, pred[]{:T(512)} %bitcast.16, pred[]{:T(512)} %bitcast.20), kind=kLoop, calls=%fused_computation.1 | loop fusion | flops 2048000 | bytes 9830403 | tf_op jit(solution)/shard_map/jit(_where)/select_n | solution.py:309
  103.1 2.2 fusion.164
  105.8 1.1 copy.112
  108.0 1.1 fusion.5
  111.2 1.1 fusion.2
  112.9 4.3 fusion.165
  117.4 29.3 %all-gather.10.cloned.1.call-done = bf16[1280,640]{0,1:T(8,128)(2,1)} async-done(((bf16[1280,160]{0,1:T(8,128)(2,1)}), bf16[1280,640]{0,1:T(8,128)(2,1)}) %all-gather.10.cloned.1.call-update) | async-done | bytes 1638416 | tf_op jit(solution)/shard_map/all_gather | solution.py:89
  146.8 2.3 convolution_add_fusion.1
  152.7 1.5 fusion
  154.4 1.1 multiply_reduce_fusion.3
  155.5 1.1 stack.21
  156.6 1.1 stack.20
  158.8 1.1 reshape.270
  160.3 1.1 fusion.91
  161.3 4.6 %concatenate.62 = f32[64,1280]{0,1:T(8,128)} concatenate(f32[30,1280]{0,1:T(8,128)S(1)} %fusion, f32[30,1280]{0,1:T(8,128)S(1)} %fusion.150, f32[1,1280]{0,1:T(8,128)} %stack.20, f32[1,1280]{0,1:T(8,128)} %reshape.269, f32[1,1280]{0,1:T(8,128)} %reshape.270, f32[1,1280]{0,1:T(8,128)} %stack.21), dimensions={0} | concatenate | bytes 655360 | tf_op jit(solution)/shard_map/concatenate | solution.py:223
  166.6 3.4 convolution_convert_fusion
  170.1 126.9 %all-reduce.15.cloned.1.call-done = (f32[160,640]{1,0:T(8,128)}, f32[64,1280]{0,1:T(8,128)}) async-done(((f32[160,640]{1,0:T(8,128)}, f32[64,1280]{0,1:T(8,128)}), (f32[160,640]{1,0:T(8,128)}, f32[64,1280]{0,1:T(8,128)})) %all-reduce.15.cloned.1.call-update) | async-done | bytes 737296 | tf_op jit(solution)/shard_map/psum | solution.py:242
  296.9 2.3 slice.225
  299.2 2.2 slice.226
  301.4 1.4 fusion.32
  302.8 1.4 fusion.35
  306.9 1.1 stack.23
  308.0 1.1 stack.22
  309.9 1.8 fusion.55
  312.7 1.1 reshape.272
  313.9 1.1 fusion.117
  316.1 1.3 fusion.158
  317.3 16.7 %reduce-scatter.2.cloned.1.call-done = bf16[160,640]{1,0:T(8,128)(2,1)} async-done(((bf16[1280,640]{1,0:T(8,128)(2,1)}), bf16[160,640]{1,0:T(8,128)(2,1)}) %reduce-scatter.2.cloned.1.call-update) | async-done | bytes 204816 | tf_op jit(solution)/shard_map/reduce_scatter | solution.py:239
  334.1 1.7 fusion.105
  337.9 4.8 %concatenate.65 = f32[68,1280]{0,1:T(8,128)} concatenate(f32[30,1280]{0,1:T(8,128)} %get-tuple-element.155, f32[30,1280]{0,1:T(8,128)} %get-tuple-element.154, f32[1,1280]{0,1:T(8,128)} %reshape.271, f32[1,1280]{0,1:T(8,128)} %reshape.272, f32[3,1280]{0,1:T(8,128)} %slice.225, f32[1,1280]{0,1:T(8,128)} %stack.22, f32[1,1280]{0,1:T(8,128)} %stack.23, f32[1,1280]{0,1:T(8,128)} %slice.226), dimensions={0} | concatenate | bytes 696320 | tf_op jit(solution)/shard_map/concatenate | solution.py:259
  342.7 1.3 multiply_reduce_fusion.12
  344.0 33.6 %all-reduce.13.cloned.1.call-done = bf16[160,640]{1,0:T(8,128)(2,1)} async-done(((bf16[160,640]{1,0:T(8,128)(2,1)}), bf16[160,640]{1,0:T(8,128)(2,1)}) %all-reduce.13.cloned.1.call-update) | async-done | bytes 204816 | tf_op jit(solution)/shard_map/psum | solution.py:238
  380.6 40.0 %all-reduce.8 = (f32[]{:T(128)}, f32[]{:T(128)}, f32[]{:T(128)}) all-reduce(f32[]{:T(128)} %get-tuple-element.126, f32[]{:T(128)} %get-tuple-element.125, f32[]{:T(128)S(6)} %add.335), channel_id=1, replica_groups=mesh['dp'=4,'fsdp'=8] {'dp','fsdp'}, use_global_device_ids=true, to_apply=%region_22.23 | all-reduce | flops 3 | bytes 24 | tf_op jit(solution)/shard_map/psum | solution.py:242
  424.7 4.8 %fusion.17 = (f32[400,640]{1,0:T(8,128)S(1)}, f32[400,640]{1,0:T(8,128)S(1)}) fusion(f32[400,640]{1,0:T(8,128)} %param.30, f32[400,640]{1,0:T(8,128)} %param.29, f32[640,640]{1,0:T(8,128)S(1)} %get-tuple-element.151, f32[400,640]{1,0:T(8,128)S(1)} %fusion.105, f32[]{:T(128)S(6)} %div.159), kind=kOutput, calls=%fused_computation.48 | convolution fusion | flops 1968128000 | bytes 6758404 | tf_op jit(solution)/shard_map/dot_general | solution.py:97
  429.6 1.4 fusion.73
  431.0 1.4 fusion.170
  432.5 2.4 fusion.169
  434.9 1.4 fusion.72
  436.4 1.4 fusion.168
  437.9 1.4 fusion.151
  (193 shorter events, 27.0 us)
Async XLA Ops:
  7.2 19.0 %copy-start.23 = (f32[400,160]{0,1:T(8,128)S(1)}, f32[400,160]{0,1:T(8,128)}, u32[]{:S(2)}) copy-start(f32[400,160]{0,1:T(8,128)} %param.24) | copy-start | bytes 768004
  7.2 95.8 %all-gather.6.cloned.1.call-start = ((), (), s32[]{:S(2)}) async-start(), calls=%async_computation.1 | async-start | bytes 2048000 | tf_op jit(solution)/shard_map/all_gather | solution.py:87
  26.2 86.8 %all-gather.8.cloned.1.call-start = ((), (), s32[]{:S(2)}) async-start(), calls=%async_computation.2 | async-start | bytes 5120000 | tf_op jit(solution)/shard_map/all_gather | solution.py:88
  46.0 2.5 copy-start.25
  48.4 16.3 %copy-start.33 = (s32[2,1024]{1,0:T(2,128)S(1)}, s32[2,1024]{1,0:T(2,128)}, u32[]{:S(2)}) copy-start(s32[2,1024]{1,0:T(2,128)} %param.20) | copy-start | bytes 24580
  48.4 16.4 %copy-start.34 = (s32[2,1024]{1,0:T(2,128)S(1)}, s32[2,1024]{1,0:T(2,128)}, u32[]{:S(2)}) copy-start(s32[2,1024]{1,0:T(2,128)} %param.19) | copy-start | bytes 24580
  48.5 98.3 %all-gather.10.cloned.1.call-start = ((), (), s32[]{:S(2)}) async-start(), calls=%async_computation.3 | async-start | bytes 2048000 | tf_op jit(solution)/shard_map/all_gather | solution.py:89
  64.6 232.3 %all-reduce.15.cloned.1.call-start = ((), (), s32[]{:S(2)}) async-start(), calls=%async_computation.6 | async-start | bytes 2129920 | tf_op jit(solution)/shard_map/psum | solution.py:242
  90.8 1.7 copy-start.36
  90.8 1.7 copy-start.31
  90.8 4.4 copy-start.35
  98.2 4.8 %copy-start.10 = (bf16[32,1280]{0,1:T(8,128)(2,1)}, bf16[32,1280]{0,1:T(8,128)(2,1)S(1)}, u32[]{:S(2)}) copy-start(bf16[32,1280]{0,1:T(8,128)(2,1)S(1)} %fusion.52) | copy-start | bytes 245764
  105.4 1.5 copy-start.42
  105.4 1.5 copy-start.37
  117.2 31.9 %copy-start.6 = (f32[256,640]{1,0:T(8,128)}, f32[256,640]{1,0:T(8,128)S(1)}, u32[]{:S(2)}) copy-start(f32[256,640]{1,0:T(8,128)S(1)} %get-tuple-element.179) | copy-start | bytes 1966084
  149.9 0.9 copy-start.32
  152.5 1.7 copy-start.7
  152.5 1.9 copy-start.44
  152.7 2.8 copy-start.14
  165.9 168.1 %reduce-scatter.2.cloned.1.call-start = ((), (), s32[]{:S(2)}) async-start(), calls=%async_computation.4 | async-start | bytes 1843200 | tf_op jit(solution)/shard_map/reduce_scatter | solution.py:239
  170.0 207.6 %all-reduce.13.cloned.1.call-start = ((), (), s32[]{:S(2)}) async-start(), calls=%async_computation.5 | async-start | bytes 409600 | tf_op jit(solution)/shard_map/psum | solution.py:238
  296.9 4.5 copy-start.5
  296.9 7.3 %copy-start = (bf16[3200,640]{0,1:T(8,128)(2,1)S(1)}, bf16[3200,640]{0,1:T(8,128)(2,1)}, u32[]{:S(2)}) copy-start(bf16[3200,640]{0,1:T(8,128)(2,1)} %all-gather.8.cloned.1.call-done) | copy-start | bytes 12288004
  305.3 0.8 copy-start.38
  306.1 3.0 copy-start.2
  311.6 4.1 copy-start.41
  312.7 3.3 copy-start.1
  315.0 0.8 copy-start.8
  424.6 4.9 %copy-start.3 = (f32[640,640]{1,0:T(8,128)S(1)}, f32[640,640]{1,0:T(8,128)}, u32[]{:S(2)}) copy-start(f32[640,640]{1,0:T(8,128)} %get-tuple-element.149) | copy-start | bytes 4915204
  424.6 4.9 %copy-start.13 = (bf16[160,640]{1,0:T(8,128)(2,1)S(1)}, bf16[160,640]{1,0:T(8,128)(2,1)}, u32[]{:S(2)}) copy-start(bf16[160,640]{1,0:T(8,128)(2,1)} %all-reduce.13.cloned.1.call-done) | copy-start | bytes 614404
  424.7 4.9 %copy-start.15 = (f32[160,640]{1,0:T(8,128)S(1)}, f32[160,640]{1,0:T(8,128)}, u32[]{:S(2)}) copy-start(f32[160,640]{1,0:T(8,128)} %param.32) | copy-start | bytes 1228804
  424.7 4.9 %copy-start.16 = (f32[160,640]{1,0:T(8,128)S(1)}, f32[160,640]{1,0:T(8,128)}, u32[]{:S(2)}) copy-start(f32[160,640]{1,0:T(8,128)} %param.31) | copy-start | bytes 1228804
  429.5 3.0 copy-start.11
  429.5 3.0 copy-start.12
  429.5 1.5 copy-start.26
  431.0 1.5 copy-start.19
  431.0 1.5 copy-start.20
  431.0 1.4 copy-start.24
  432.5 2.4 copy-start.4
  432.5 2.4 copy-start.9
  432.5 2.4 copy-start.17
  432.5 2.4 copy-start.18
  434.9 1.4 copy-start.27
  436.3 1.5 copy-start.21
  436.4 1.5 copy-start.22
  436.4 1.5 copy-start.29
  436.4 1.5 copy-start.30
  436.4 1.5 copy-start.39
  (3 other events, 2.0 us)
Sparse Core Ops, SparseCore 0:
  26.3 32.3 all-gather.5
  61.1 51.7 all-gather.7
  115.3 31.3 all-gather.9
  166.0 130.8 all-reduce.14
  299.1 34.9 reduce-scatter.1
  336.9 40.6 all-reduce.12
where the time goes:
time: 454 us; the launch traced here: 449 us
  waiting for transfers between devices  207 us (46%)
  blocking collectives  114 us (25%)
  matrix products  46.6 us (10%)
  local copies, waits for them, and re-layouts  34.3 us (8%)
  between operations  27 us (6%)
  other arithmetic  18.8 us (4%)
    psum x1, waiting for transfers between devices, local(): lax.psum((tap_grads, wide_rows, summed_loss, slot_count), ('dp', 'fsdp'))  127 us
    psum x1, blocking collectives, local(): lax.psum((tap_grads, wide_rows, summed_loss, slot_count), ('dp', 'fsdp'))  40 us
    psum x1, waiting for transfers between devices, local(): lax.psum(lax.psum_scatter(out_grad.astype(jnp.bfloat16), 'fsdp', scatter_...  33.6 us
    all_gather x1, waiting for transfers between devices, gathered_weights(): lax.all_gather(parted[2], 'dp', axis=1, tiled=True)  29.3 us
    all_gather x1, blocking collectives, gathered_weights(): lax.all_gather(shards[1], 'fsdp', axis=0, tiled=True)  19 us
    all_gather x1, blocking collectives, gathered_weights(): lax.all_gather(shards[0], 'fsdp', axis=0, tiled=True)  17 us
    reduce_scatter x1, waiting for transfers between devices, local(): lax.psum_scatter(out_grad.astype(jnp.bfloat16), 'fsdp', scatter_dimension...  16.7 us
    all_gather x1, blocking collectives, gathered_weights(): lax.all_gather(shards[2], 'fsdp', axis=0, tiled=True)  15.1 us
  transfers between devices with their start and end apart: 6, of which 5 were waited for; matrix products, arithmetic and copies ran while one was open for 14% of the time, Pallas kernels for 0%

commit v1 on v0

--- a/solution.py
+++ b/solution.py
@@ -17,6 +17,11 @@
 clip_limit = 0.02
 norm_eps = 1e-05
 highest_precision = lax.Precision.HIGHEST
+
+
+def gather_and_add(shard, axis):
+    shards = lax.all_gather(shard, axis)
+    return jnp.sum(shards, axis=0)
 
 
 def layer_norm(values, norm_gain, norm_bias):
@@ -235,7 +240,7 @@
         ],
         axis=0,
     )
-    out_rows = lax.psum(
+    out_rows = gather_and_add(
         lax.psum_scatter(out_grad.astype(jnp.bfloat16), "fsdp", scatter_dimension=0, tiled=True),
         "dp",
     ).astype(jnp.float32)

time: 454 us -> 421 us (0.927)
  waiting for transfers between devices: 207 us -> 163 us
  blocking collectives: 114 us -> 124 us
    psum x1 -> x0, waiting for transfers between devices: 33.6 us -> none  [local(): lax.psum(lax.psum_scatter(out_grad.astype(jnp.bfloat16), 'fsdp', scatter_...]
    all_gather x0 -> x1, blocking collectives: none -> 12.4 us  [gather_and_add(): shards = lax.all_gather(shard, axis)]
    reduce_scatter x1, waiting for transfers between devices: 16.7 us -> 5.59 us  [local(): lax.psum_scatter(out_grad.astype(jnp.bfloat16), 'fsdp', scatter_dimension...]
  transfers between devices with their start and end apart: 6 -> 5, of which waited for: 5 -> 4; matrix products, arithmetic and copies ran while one was open for 14% -> 15% of each run, Pallas kernels for 0% -> 0%
where the time goes in v1:
time: 421 us; the launch traced here: 415 us
  waiting for transfers between devices  163 us (39%)
  blocking collectives  124 us (29%)
  matrix products  48.6 us (12%)
  local copies, waits for them, and re-layouts  34.2 us (8%)
  between operations  26.7 us (6%)
  other arithmetic  18.4 us (4%)
    psum x1, waiting for transfers between devices, local(): lax.psum((tap_grads, wide_rows, summed_loss, slot_count), ('dp', 'fsdp'))  127 us
    psum x1, blocking collectives, local(): lax.psum((tap_grads, wide_rows, summed_loss, slot_count), ('dp', 'fsdp'))  37.4 us
    all_gather x1, waiting for transfers between devices, gathered_weights(): lax.all_gather(parted[2], 'dp', axis=1, tiled=True)  29.3 us
    all_gather x1, blocking collectives, gathered_weights(): lax.all_gather(shards[1], 'fsdp', axis=0, tiled=True)  19 us
    all_gather x1, blocking collectives, gathered_weights(): lax.all_gather(shards[0], 'fsdp', axis=0, tiled=True)  17 us
    all_gather x1, blocking collectives, gathered_weights(): lax.all_gather(shards[2], 'fsdp', axis=0, tiled=True)  15.1 us
    all_gather x1, blocking collectives, gathered_weights(): lax.all_gather(shards[3], 'fsdp', axis=1, tiled=True)  13.9 us
    all_gather x1, blocking collectives, gather_and_add(): shards = lax.all_gather(shard, axis)  12.4 us
  transfers between devices with their start and end apart: 5, of which 4 were waited for; matrix products, arithmetic and copies ran while one was open for 15% of the time, Pallas kernels for 0%

profile of v1, /device:TPU:0, one launch (start us, length us, event | category | flops | bytes accessed | tf_op | source)
XLA Modules:
  0.0 414.9 jit_solution(5078676835497895429)
XLA Ops:
  8.2 17.0 %all_gather.32 = bf16[1280,160]{1,0:T(8,128)(2,1)S(1)} all-gather(bf16[160,160]{1,0:T(8,128)(2,1)S(1)} %convert_element_type.161), channel_id=1, replica_groups=mesh['dp'=4,'fsdp'=8] {'fsdp'}, dimensions={0}, use_global_device_ids=true | all-gather | bytes 460800 | tf_op jit(solution)/shard_map/all_gather | solution.py:86
  26.2 19.0 %all-gather.2 = bf16[8,400,160]{1,2,0:T(8,128)(2,1)S(1)} all-gather(bf16[1,400,160]{1,2,0:T(8,128)(2,1)S(1)} %convert_bitcast_fusion), channel_id=1, replica_groups=mesh['dp'=4,'fsdp'=8] {'fsdp'}, dimensions={0}, use_global_device_ids=true | all-gather | bytes 1152000 | tf_op jit(solution)/shard_map/all_gather | solution.py:87
  46.0 2.4 reshape.269
  48.5 15.1 %all_gather.36 = bf16[1280,160]{1,0:T(8,128)(2,1)S(1)} all-gather(bf16[160,160]{1,0:T(8,128)(2,1)S(1)} %convert_element_type.170), channel_id=1, replica_groups=mesh['dp'=4,'fsdp'=8] {'fsdp'}, dimensions={0}, use_global_device_ids=true | all-gather | bytes 460800 | tf_op jit(solution)/shard_map/all_gather | solution.py:88
  65.4 13.9 %all_gather.30 = bf16[68,320]{0,1:T(8,128)(2,1)S(1)} all-gather(bf16[68,40]{0,1:T(8,128)(2,1)S(1)} %convert_element_type.157), channel_id=1, replica_groups=mesh['dp'=4,'fsdp'=8] {'fsdp'}, dimensions={1}, use_global_device_ids=true | all-gather | bytes 48960 | tf_op jit(solution)/shard_map/all_gather | solution.py:89
  79.4 9.3 %all-gather.1 = bf16[4,320,68]{1,2,0:T(8,128)(2,1)S(1)} all-gather(bf16[1,320,68]{1,2,0:T(8,128)(2,1)S(1)} %copy.91), channel_id=1, replica_groups=mesh['dp'=4,'fsdp'=8] {'dp'}, dimensions={0}, use_global_device_ids=true | all-gather | bytes 217600 | tf_op jit(solution)/shard_map/all_gather | solution.py:95
  89.0 1.8 slice_reduce_fusion.1
  90.9 1.1 slice_reduce_fusion.6
  98.2 4.6 %convert_select_fusion = (f32[640,640]{1,0:T(8,128)}, f32[640,640]{1,0:T(8,128)}, f32[640,640]{1,0:T(8,128)S(1)}) fusion(f32[3,640,640]{2,1,0:T(8,128)} %param.35, pred[]{:T(512)} %bitcast.23, pred[]{:T(512)} %bitcast.17, pred[]{:T(512)} %bitcast.21), kind=kLoop, calls=%fused_computation.1 | loop fusion | flops 2048000 | bytes 9830403 | tf_op jit(solution)/shard_map/jit(_where)/select_n | solution.py:314
  103.1 2.2 fusion.164
  105.8 1.1 copy.112
  108.0 1.1 fusion.5
  111.2 1.1 fusion.2
  112.9 4.3 %fusion.165 = (f32[256]{0:T(256)S(1)}, f32[256,640]{1,0:T(8,128)S(1)}) fusion(f32[640]{0:T(1024)S(1)} %get-tuple-element.106, bf16[256,3200]{1,0:T(8,128)(2,1)} %fusion.2, bf16[3200,640]{0,1:T(8,128)(2,1)} %all-gather.9.cloned.1.call-done), kind=kOutput, calls=%fused_computation.312 | convolution fusion | flops 1048903424 | bytes 6393344 | tf_op jit(solution)/shard_map/dot_general | solution.py:189
  117.4 29.3 %all-gather.11.cloned.1.call-done = bf16[1280,640]{0,1:T(8,128)(2,1)} async-done(((bf16[1280,160]{0,1:T(8,128)(2,1)}), bf16[1280,640]{0,1:T(8,128)(2,1)}) %all-gather.11.cloned.1.call-update) | async-done | bytes 1638416 | tf_op jit(solution)/shard_map/all_gather | solution.py:94
  146.8 2.3 convolution_add_fusion.1
  152.7 1.5 fusion
  154.4 1.1 multiply_reduce_fusion.3
  155.5 1.1 stack.21
  156.6 1.1 stack.20
  158.8 1.1 reshape.271
  160.3 1.1 fusion.91
  161.3 4.6 %concatenate.62 = f32[64,1280]{0,1:T(8,128)} concatenate(f32[30,1280]{0,1:T(8,128)S(1)} %fusion, f32[30,1280]{0,1:T(8,128)S(1)} %fusion.150, f32[1,1280]{0,1:T(8,128)} %stack.20, f32[1,1280]{0,1:T(8,128)} %reshape.270, f32[1,1280]{0,1:T(8,128)} %reshape.271, f32[1,1280]{0,1:T(8,128)} %stack.21), dimensions={0} | concatenate | bytes 655360 | tf_op jit(solution)/shard_map/concatenate | solution.py:228
  166.6 3.4 convolution_convert_fusion
  170.0 126.9 %all-reduce.12.cloned.1.call-done = (f32[160,640]{1,0:T(8,128)}, f32[64,1280]{0,1:T(8,128)}) async-done(((f32[160,640]{1,0:T(8,128)}, f32[64,1280]{0,1:T(8,128)}), (f32[160,640]{1,0:T(8,128)}, f32[64,1280]{0,1:T(8,128)})) %all-reduce.12.cloned.1.call-update) | async-done | bytes 737296 | tf_op jit(solution)/shard_map/psum | solution.py:247
  296.9 1.5 slice.225
  298.4 2.2 slice.226
  300.6 1.4 fusion.32
  302.0 1.4 fusion.35
  306.1 1.1 stack.23
  307.2 1.1 stack.22
  309.1 2.3 fusion.55
  312.5 1.1 reshape.273
  313.6 1.1 fusion.117
  315.5 1.8 fusion.105
  320.4 1.4 fusion.153
  321.8 1.3 fusion.158
  323.1 4.3 %concatenate.65 = f32[68,1280]{0,1:T(8,128)S(1)} concatenate(f32[30,1280]{0,1:T(8,128)} %get-tuple-element.155, f32[30,1280]{0,1:T(8,128)} %get-tuple-element.154, f32[1,1280]{0,1:T(8,128)} %reshape.272, f32[1,1280]{0,1:T(8,128)} %reshape.273, f32[3,1280]{0,1:T(8,128)S(1)} %slice.225, f32[1,1280]{0,1:T(8,128)} %stack.22, f32[1,1280]{0,1:T(8,128)} %stack.23, f32[1,1280]{0,1:T(8,128)} %slice.226), dimensions={0} | concatenate | bytes 696320 | tf_op jit(solution)/shard_map/concatenate | solution.py:264
  328.2 5.6 %reduce-scatter.2.cloned.1.call-done = bf16[160,640]{1,0:T(8,128)(2,1)} async-done(((bf16[1280,640]{1,0:T(8,128)(2,1)}), bf16[160,640]{1,0:T(8,128)(2,1)}) %reduce-scatter.2.cloned.1.call-update) | async-done | bytes 204816 | tf_op jit(solution)/shard_map/reduce_scatter | solution.py:244
  333.8 12.4 %all-gather = bf16[640,640]{1,0:T(8,128)(2,1)S(1)} all-gather(bf16[160,640]{1,0:T(8,128)(2,1)} %reduce-scatter.2.cloned.1.call-done), channel_id=2, replica_groups=mesh['dp'=4,'fsdp'=8] {'dp'}, dimensions={0}, use_global_device_ids=true | all-gather | bytes 1024000 | tf_op jit(solution)/shard_map/all_gather | solution.py:23
  348.4 37.4 %all-reduce.8 = (f32[]{:T(128)}, f32[]{:T(128)}, f32[]{:T(128)}) all-reduce(f32[]{:T(128)} %get-tuple-element.126, f32[]{:T(128)} %get-tuple-element.125, f32[]{:T(128)S(6)} %add.333), channel_id=1, replica_groups=mesh['dp'=4,'fsdp'=8] {'dp','fsdp'}, use_global_device_ids=true, to_apply=%region_22.23 | all-reduce | flops 3 | bytes 24 | tf_op jit(solution)/shard_map/psum | solution.py:247
  389.9 3.1 fusion.73
  393.0 3.2 fusion.17
  396.3 2.8 fusion.170
  399.2 2.4 fusion.169
  401.6 1.4 fusion.72
  403.0 1.4 fusion.168
  404.5 1.4 fusion.151
  (196 shorter events, 27.6 us)
Async XLA Ops:
  7.2 19.0 %copy-start.25 = (f32[400,160]{0,1:T(8,128)S(1)}, f32[400,160]{0,1:T(8,128)}, u32[]{:S(2)}) copy-start(f32[400,160]{0,1:T(8,128)} %param.24) | copy-start | bytes 768004
  7.2 95.9 %all-gather.7.cloned.1.call-start = ((), (), s32[]{:S(2)}) async-start(), calls=%async_computation.1 | async-start | bytes 2048000 | tf_op jit(solution)/shard_map/all_gather | solution.py:92
  26.2 86.8 %all-gather.9.cloned.1.call-start = ((), (), s32[]{:S(2)}) async-start(), calls=%async_computation.2 | async-start | bytes 5120000 | tf_op jit(solution)/shard_map/all_gather | solution.py:93
  46.0 2.5 copy-start.27
  48.4 16.3 %copy-start.35 = (s32[2,1024]{1,0:T(2,128)S(1)}, s32[2,1024]{1,0:T(2,128)}, u32[]{:S(2)}) copy-start(s32[2,1024]{1,0:T(2,128)} %param.20) | copy-start | bytes 24580
  48.4 16.4 %copy-start.36 = (s32[2,1024]{1,0:T(2,128)S(1)}, s32[2,1024]{1,0:T(2,128)}, u32[]{:S(2)}) copy-start(s32[2,1024]{1,0:T(2,128)} %param.19) | copy-start | bytes 24580
  48.5 98.3 %all-gather.11.cloned.1.call-start = ((), (), s32[]{:S(2)}) async-start(), calls=%async_computation.3 | async-start | bytes 2048000 | tf_op jit(solution)/shard_map/all_gather | solution.py:94
  64.6 232.3 %all-reduce.12.cloned.1.call-start = ((), (), s32[]{:S(2)}) async-start(), calls=%async_computation.5 | async-start | bytes 2129920 | tf_op jit(solution)/shard_map/psum | solution.py:247
  90.8 1.7 copy-start.38
  90.8 1.7 copy-start.33
  90.8 4.4 %copy-start.37 = (s32[3]{0:T(128)S(1)}, s32[3]{0:T(128)}, u32[]{:S(2)}) copy-start(s32[3]{0:T(128)} %param.36) | copy-start | bytes 40
  98.2 4.9 %copy-start.11 = (bf16[32,1280]{0,1:T(8,128)(2,1)}, bf16[32,1280]{0,1:T(8,128)(2,1)S(1)}, u32[]{:S(2)}) copy-start(bf16[32,1280]{0,1:T(8,128)(2,1)S(1)} %fusion.52) | copy-start | bytes 245764
  105.5 1.5 copy-start.44
  105.5 1.5 copy-start.39
  117.2 31.9 %copy-start.7 = (f32[256,640]{1,0:T(8,128)}, f32[256,640]{1,0:T(8,128)S(1)}, u32[]{:S(2)}) copy-start(f32[256,640]{1,0:T(8,128)S(1)} %get-tuple-element.179) | copy-start | bytes 1966084
  149.9 0.9 copy-start.34
  152.5 1.7 copy-start.8
  152.5 1.9 copy-start.46
  152.7 2.8 copy-start.17
  165.9 167.9 %reduce-scatter.2.cloned.1.call-start = ((), (), s32[]{:S(2)}) async-start(), calls=%async_computation.4 | async-start | bytes 1843200 | tf_op jit(solution)/shard_map/reduce_scatter | solution.py:244
  296.9 3.7 copy-start.6
  296.9 6.5 %copy-start = (bf16[3200,640]{0,1:T(8,128)(2,1)S(1)}, bf16[3200,640]{0,1:T(8,128)(2,1)}, u32[]{:S(2)}) copy-start(bf16[3200,640]{0,1:T(8,128)(2,1)} %all-gather.9.cloned.1.call-done) | copy-start | bytes 12288004
  304.8 1.0 copy-start.45
  305.3 3.0 copy-start.2
  312.5 7.9 %copy-start.43 = (f32[32]{0:T(128)S(1)}, f32[32]{0:T(128)}, u32[]{:S(2)}) copy-start(f32[32]{0:T(128)} %copy-done.42) | copy-start | bytes 388
  315.5 6.2 %copy-start.1 = (f32[64,1280]{0,1:T(8,128)S(1)}, f32[64,1280]{0,1:T(8,128)}, u32[]{:S(2)}) copy-start(f32[64,1280]{0,1:T(8,128)} %get-tuple-element.131) | copy-start | bytes 983044
  317.3 1.0 copy-start.4
  327.4 0.8 copy-start.16
  327.4 62.5 %copy-start.18 = (f32[160,640]{1,0:T(8,128)S(1)}, f32[160,640]{1,0:T(8,128)}, u32[]{:S(2)}) copy-start(f32[160,640]{1,0:T(8,128)} %param.32) | copy-start | bytes 1228804
  389.9 3.1 copy-start.5
  389.9 3.1 copy-start.12
  389.9 3.1 copy-start.13
  393.0 3.3 copy-start.21
  393.0 3.3 copy-start.22
  393.0 3.2 copy-start.28
  396.2 2.9 copy-start.14
  396.2 2.9 copy-start.15
  396.3 2.8 copy-start.26
  399.1 2.4 copy-start.3
  399.1 2.4 copy-start.10
  399.1 2.4 copy-start.19
  399.1 2.4 copy-start.20
  401.6 1.4 copy-start.29
  403.0 1.5 copy-start.23
  403.0 1.5 copy-start.24
  403.0 1.5 copy-start.31
  403.0 1.5 copy-start.32
  403.0 1.5 copy-start.41
  (4 other events, 2.8 us)
Sparse Core Ops, SparseCore 0:
  26.3 32.3 all-gather.6
  61.1 51.7 all-gather.8
  115.3 31.3 all-gather.10
  166.0 130.8 all-reduce.11
  299.1 34.6 reduce-scatter.1
